TPU v7x, 32 devices: a whole 2x2x4 slice. The times are simulated.
32 devices in a mesh: seq: 8 (over z, x), tp: 4 (over y, core).
Axes of the slice: x: 2, y: 2, z: 4, core: 2. Of those that a mesh axis runs over, the one named last changes fastest.
Arguments:
- query_rows: bfloat16 [1536, 4096], P('seq', 'tp'), may hold values from -120 to 120
- key_rows: bfloat16 [1536, 1024], P('seq', 'tp'), may hold values from -6 to 6
- value_rows: bfloat16 [1536, 1024], P('seq', 'tp'), may hold values from -6 to 6
- document_ids: int32 [1536], replicated, may hold values from 0 to 3, never falling along the last dimension, each value on 1 to 768 neighbouring positions
- output_weight: bfloat16 [4096, 8192], P('tp'), may hold values from -0.09375 to 0.09375
Outputs:
- attended: bfloat16 [1536, 8192], P(('seq', 'tp'))
Inputs may be any that keep to these rules, and one draw needn't show every extreme that they name: `document_ids`: never falling along the sequence; every document holds at most 768 tokens, and one holds exactly 768.
All inputs are finite; a program needn't handle non-finite values.
Results may differ from a plain program's by a relative error of at most 0.014.
Values may be sent and summed in bfloat16 or wider, within the bound.
A program may use at most 64 MiB of HBM per device.

v0:
```python
import jax
import jax.numpy as jnp
from jax import lax
from jax.sharding import PartitionSpec as P

HEADS = 32
KV = 8
HD = 128


def shifted(block, axis, distance):
    devices = range(lax.axis_size(axis))
    route = [(i - distance, i) for i in devices if i - distance in devices]
    return lax.ppermute(block, axis, route)


def per_device(query_rows, key_rows, value_rows, document_ids, output_weight):
    tokens = query_rows.shape[0]
    kv_local = key_rows.shape[1] // HD
    group = HEADS // KV
    seq_total = document_ids.shape[0]
    scaling = 1.0 / HD**0.5
    reach = min(12, lax.axis_size("seq") // 2)
    first_row = lax.axis_index("seq") * tokens
    queries = query_rows.reshape(tokens, kv_local, group, HD)
    query_doc = lax.dynamic_slice_in_dim(document_ids, first_row, tokens, 0)
    query_pos = first_row + jnp.arange(tokens, dtype=jnp.int32)

    def attend_block(state_in, key_block, value_block, offset):
        key_count = key_block.shape[0]
        padded_doc = jnp.concatenate([jnp.full((key_count,), -1, jnp.int32), document_ids], axis=0)
        doc_start = jnp.clip(offset + key_count, 0, seq_total)
        key_doc = lax.dynamic_slice_in_dim(padded_doc, doc_start, key_count, 0)
        key_pos = offset + jnp.arange(key_count, dtype=jnp.int32)
        allowed = (
            (key_doc[None, :] == query_doc[:, None])
            & (key_pos[None, :] <= query_pos[:, None])
            & (key_pos[None, :] >= 0)
        )
        running_max, running_sum, accumulated = state_in
        scores = (
            jnp.einsum(
                "tkgd,ukd->kgtu",
                queries,
                key_block.reshape(key_count, kv_local, HD),
                preferred_element_type=jnp.float32,
            )
            * scaling
        )
        scores = jnp.where(allowed, scores, -jnp.inf)
        new_max = jnp.maximum(running_max, jnp.max(scores, axis=-1))
        exponent = jnp.exp(scores - new_max[..., None])
        rescale = jnp.exp(running_max - new_max)
        new_sum = running_sum * rescale + jnp.sum(exponent, axis=-1)
        added = jnp.einsum(
            "kgtu,ukd->kgtd",
            exponent.astype(jnp.bfloat16),
            value_block.reshape(key_count, kv_local, HD),
            preferred_element_type=jnp.float32,
        )
        return (new_max, new_sum, accumulated * rescale[..., None] + added)

    initial = (
        jnp.full((kv_local, group, tokens), -1e30, jnp.float32),
        jnp.zeros((kv_local, group, tokens), jnp.float32),
        jnp.zeros((kv_local, group, tokens, HD), jnp.float32),
    )
    own_state = attend_block(initial, key_rows, value_rows, first_row)

    def turn(turn_index, carried):
        current, key_block, value_block = carried
        key_block, value_block = shifted((key_block, value_block), "seq", 1)
        offset = first_row - (turn_index + 1) * tokens
        current = attend_block(current, key_block, value_block, offset)
        return (current, key_block, value_block)

    final_state = lax.fori_loop(0, reach, turn, (own_state, key_rows, value_rows))[0]
    running_max, running_sum, accumulated = final_state
    context = accumulated / running_sum[..., None]
    context = (
        context.transpose(2, 0, 1, 3).reshape(tokens, kv_local * group * HD).astype(jnp.bfloat16)
    )
    return lax.psum_scatter(
        jnp.dot(context, output_weight, preferred_element_type=jnp.float32).astype(jnp.bfloat16),
        "tp",
        scatter_dimension=0,
        tiled=True,
    )


def solution(mesh):
    in_specs = (P("seq", "tp"), P("seq", "tp"), P("seq", "tp"), P(), P("tp", None))
    out_specs = P(("seq", "tp"), None)
    return jax.shard_map(
        per_device, mesh=mesh, in_specs=in_specs, out_specs=out_specs, check_vma=False
    )
```

profile of v0, /device:TPU:17, one launch (start us, length us, event | category | flops | bytes accessed | tf_op | source)
XLA Modules:
  0.0 114.7 jit_solution(3937121556764388139)
XLA Ops:
  6.5 0.9 copy.73
  7.4 0.9 copy.74
  8.4 1.3 %reshape.61 = bf16[192,2,4,128]{3,2,1,0:T(4,128)(2,1)S(1)} reshape(bf16[192,1024]{1,0:T(8,128)(2,1)} %param.7) | data formatting | bytes 786432 | tf_op jit(solution)/shard_map/reshape | solution.py:25
  10.0 0.4 fusion.18
  10.7 0.6 convolution_add_fusion.1
  11.3 43.4 %while.23 = (s32[]{:T(128)}, f32[2,4,192]{2,1,0:T(4,128)S(1)}, f32[2,4,192]{2,1,0:T(4,128)S(1)}, f32[2,4,192,128]{3,2,1,0:T(8,128)S(1)}, bf16[192,256]{1,0:T(8,1...) while((s32[]{:T(128)}, f32[2,4,192]{2,1,0:T(4,128)S(1)}, ...), condition=%wide.region_5.6_spmd.clone.clone, body=%wide.region_2.5_spmd.clone.clone.sunk | while | flops 153603840 | bytes 7458721 | solution.py:77
  11.3 3.1 %collective-permute-start.1 = (bf16[192,256]{1,0:T(8,128)(2,1)S(1)}, bf16[192,256]{1,0:T(8,128)(2,1)S(1)}, u32[]{:S(2)}, u32[]{:S(2)}) collective-permute-start(bf16[192,256]{1,0:T(8,128)(2,1)S(1)} %get-tuple-element.380), channel_id=1, source_target_pairs={{0,4},{4,8},{8,12},{12,16},{16,20},{20,24},{24,28},{1,5},{5,9},{9,... | collective-permute-start | bytes 294920 | tf_op jit(solution)/shard_map/while/body/eval_jaxpr/ppermute | solution.py:14
  14.4 3.2 %collective-permute-start = (bf16[192,256]{1,0:T(8,128)(2,1)S(1)}, bf16[192,256]{1,0:T(8,128)(2,1)S(1)}, u32[]{:S(2)}, u32[]{:S(2)}) collective-permute-start(bf16[192,256]{1,0:T(8,128)(2,1)S(1)} %get-tuple-element.379), channel_id=1, source_target_pairs={{0,4},{4,8},{8,12},{12,16},{16,20},{20,24},{24,28},{1,5},{5,9},{9,... | collective-permute-start | bytes 294920 | tf_op jit(solution)/shard_map/while/body/eval_jaxpr/ppermute | solution.py:14
  17.9 2.8 %collective-permute-done = bf16[192,256]{1,0:T(8,128)(2,1)S(1)} collective-permute-done((bf16[192,256]{1,0:T(8,128)(2,1)S(1)}, bf16[192,256]{1,0:T(8,128)(2,1)S(1)}, u32[]{:S(2)}, u32[]{:S(2)}) %collective-permute-start) | collective-permute-done | bytes 98336 | tf_op jit(solution)/shard_map/while/body/eval_jaxpr/ppermute | solution.py:14
  21.5 0.7 convolution_add_fusion.3
  22.3 2.3 %collective-permute-start.1 = (bf16[192,256]{1,0:T(8,128)(2,1)S(1)}, bf16[192,256]{1,0:T(8,128)(2,1)S(1)}, u32[]{:S(2)}, u32[]{:S(2)}) collective-permute-start(bf16[192,256]{1,0:T(8,128)(2,1)S(1)} %get-tuple-element.380), channel_id=1, source_target_pairs={{0,4},{4,8},{8,12},{12,16},{16,20},{20,24},{24,28},{1,5},{5,9},{9,... | collective-permute-start | bytes 294920 | tf_op jit(solution)/shard_map/while/body/eval_jaxpr/ppermute | solution.py:14
  24.6 4.0 %collective-permute-start = (bf16[192,256]{1,0:T(8,128)(2,1)S(1)}, bf16[192,256]{1,0:T(8,128)(2,1)S(1)}, u32[]{:S(2)}, u32[]{:S(2)}) collective-permute-start(bf16[192,256]{1,0:T(8,128)(2,1)S(1)} %get-tuple-element.379), channel_id=1, source_target_pairs={{0,4},{4,8},{8,12},{12,16},{16,20},{20,24},{24,28},{1,5},{5,9},{9,... | collective-permute-start | bytes 294920 | tf_op jit(solution)/shard_map/while/body/eval_jaxpr/ppermute | solution.py:14
  28.9 3.0 %collective-permute-done = bf16[192,256]{1,0:T(8,128)(2,1)S(1)} collective-permute-done((bf16[192,256]{1,0:T(8,128)(2,1)S(1)}, bf16[192,256]{1,0:T(8,128)(2,1)S(1)}, u32[]{:S(2)}, u32[]{:S(2)}) %collective-permute-start) | collective-permute-done | bytes 98336 | tf_op jit(solution)/shard_map/while/body/eval_jaxpr/ppermute | solution.py:14
  32.7 0.7 convolution_add_fusion.3
  33.4 2.1 %collective-permute-start.1 = (bf16[192,256]{1,0:T(8,128)(2,1)S(1)}, bf16[192,256]{1,0:T(8,128)(2,1)S(1)}, u32[]{:S(2)}, u32[]{:S(2)}) collective-permute-start(bf16[192,256]{1,0:T(8,128)(2,1)S(1)} %get-tuple-element.380), channel_id=1, source_target_pairs={{0,4},{4,8},{8,12},{12,16},{16,20},{20,24},{24,28},{1,5},{5,9},{9,... | collective-permute-start | bytes 294920 | tf_op jit(solution)/shard_map/while/body/eval_jaxpr/ppermute | solution.py:14
  35.5 3.5 %collective-permute-start = (bf16[192,256]{1,0:T(8,128)(2,1)S(1)}, bf16[192,256]{1,0:T(8,128)(2,1)S(1)}, u32[]{:S(2)}, u32[]{:S(2)}) collective-permute-start(bf16[192,256]{1,0:T(8,128)(2,1)S(1)} %get-tuple-element.379), channel_id=1, source_target_pairs={{0,4},{4,8},{8,12},{12,16},{16,20},{20,24},{24,28},{1,5},{5,9},{9,... | collective-permute-start | bytes 294920 | tf_op jit(solution)/shard_map/while/body/eval_jaxpr/ppermute | solution.py:14
  39.3 2.9 %collective-permute-done = bf16[192,256]{1,0:T(8,128)(2,1)S(1)} collective-permute-done((bf16[192,256]{1,0:T(8,128)(2,1)S(1)}, bf16[192,256]{1,0:T(8,128)(2,1)S(1)}, u32[]{:S(2)}, u32[]{:S(2)}) %collective-permute-start) | collective-permute-done | bytes 98336 | tf_op jit(solution)/shard_map/while/body/eval_jaxpr/ppermute | solution.py:14
  43.1 0.7 convolution_add_fusion.3
  43.8 3.0 %collective-permute-start.1 = (bf16[192,256]{1,0:T(8,128)(2,1)S(1)}, bf16[192,256]{1,0:T(8,128)(2,1)S(1)}, u32[]{:S(2)}, u32[]{:S(2)}) collective-permute-start(bf16[192,256]{1,0:T(8,128)(2,1)S(1)} %get-tuple-element.380), channel_id=1, source_target_pairs={{0,4},{4,8},{8,12},{12,16},{16,20},{20,24},{24,28},{1,5},{5,9},{9,... | collective-permute-start | bytes 294920 | tf_op jit(solution)/shard_map/while/body/eval_jaxpr/ppermute | solution.py:14
  46.9 1.9 %collective-permute-start = (bf16[192,256]{1,0:T(8,128)(2,1)S(1)}, bf16[192,256]{1,0:T(8,128)(2,1)S(1)}, u32[]{:S(2)}, u32[]{:S(2)}) collective-permute-start(bf16[192,256]{1,0:T(8,128)(2,1)S(1)} %get-tuple-element.379), channel_id=1, source_target_pairs={{0,4},{4,8},{8,12},{12,16},{16,20},{20,24},{24,28},{1,5},{5,9},{9,... | collective-permute-start | bytes 294920 | tf_op jit(solution)/shard_map/while/body/eval_jaxpr/ppermute | solution.py:14
  49.1 4.0 %collective-permute-done = bf16[192,256]{1,0:T(8,128)(2,1)S(1)} collective-permute-done((bf16[192,256]{1,0:T(8,128)(2,1)S(1)}, bf16[192,256]{1,0:T(8,128)(2,1)S(1)}, u32[]{:S(2)}, u32[]{:S(2)}) %collective-permute-start) | collective-permute-done | bytes 98336 | tf_op jit(solution)/shard_map/while/body/eval_jaxpr/ppermute | solution.py:14
  53.9 0.7 convolution_add_fusion.3
  55.6 10.9 %convolution_convert_fusion = bf16[192,8192]{1,0:T(8,128)(2,1)} fusion(bf16[192,1024]{1,0:T(8,128)(2,1)S(1)} %convert_element_type.25, bf16[1024,8192]{1,0:T(8,128)(2,1)} %param.11), kind=kOutput, calls=%fused_computation.16 | convolution fusion | flops 3222798336 | bytes 20316160 | tf_op jit(solution)/shard_map/dot_general | solution.py:84
  66.5 41.4 %reduce-scatter.2.cloned.1.call-done = bf16[48,8192]{1,0:T(8,128)(2,1)} async-done(((bf16[192,8192]{1,0:T(8,128)(2,1)}), bf16[48,8192]{1,0:T(8,128)(2,1)}) %reduce-scatter.2.cloned.1.call-update) | async-done | bytes 786448 | tf_op jit(solution)/shard_map/reduce_scatter | solution.py:83
  (72 shorter events, 5.6 us)
Async XLA Ops:
  6.5 3.2 %copy-start = (s32[1536]{0:T(1024)S(1)}, s32[1536]{0:T(1024)}, u32[]{:S(2)}) copy-start(s32[1536]{0:T(1024)} %param.10) | copy-start | bytes 18436
  6.5 101.3 %reduce-scatter.2.cloned.1.call-start = ((), (), s32[]{:S(2)}) async-start(), calls=%async_computation.1 | async-start | bytes 3932160 | tf_op jit(solution)/shard_map/reduce_scatter | solution.py:83
  11.3 10.2 %collective-permute-start.1 = (bf16[192,256]{1,0:T(8,128)(2,1)S(1)}, bf16[192,256]{1,0:T(8,128)(2,1)S(1)}, u32[]{:S(2)}, u32[]{:S(2)}) collective-permute-start(bf16[192,256]{1,0:T(8,128)(2,1)S(1)} %get-tuple-element.380), channel_id=1, source_target_pairs={{0,4},{4,8},{8,12},{12,16},{16,20},{20,24},{24,28},{1,5},{5,9},{9,... | collective-permute-start | bytes 294920 | tf_op jit(solution)/shard_map/while/body/eval_jaxpr/ppermute | solution.py:14
  14.4 6.3 %collective-permute-start = (bf16[192,256]{1,0:T(8,128)(2,1)S(1)}, bf16[192,256]{1,0:T(8,128)(2,1)S(1)}, u32[]{:S(2)}, u32[]{:S(2)}) collective-permute-start(bf16[192,256]{1,0:T(8,128)(2,1)S(1)} %get-tuple-element.379), channel_id=1, source_target_pairs={{0,4},{4,8},{8,12},{12,16},{16,20},{20,24},{24,28},{1,5},{5,9},{9,... | collective-permute-start | bytes 294920 | tf_op jit(solution)/shard_map/while/body/eval_jaxpr/ppermute | solution.py:14
  22.3 10.4 %collective-permute-start.1 = (bf16[192,256]{1,0:T(8,128)(2,1)S(1)}, bf16[192,256]{1,0:T(8,128)(2,1)S(1)}, u32[]{:S(2)}, u32[]{:S(2)}) collective-permute-start(bf16[192,256]{1,0:T(8,128)(2,1)S(1)} %get-tuple-element.380), channel_id=1, source_target_pairs={{0,4},{4,8},{8,12},{12,16},{16,20},{20,24},{24,28},{1,5},{5,9},{9,... | collective-permute-start | bytes 294920 | tf_op jit(solution)/shard_map/while/body/eval_jaxpr/ppermute | solution.py:14
  24.6 7.3 %collective-permute-start = (bf16[192,256]{1,0:T(8,128)(2,1)S(1)}, bf16[192,256]{1,0:T(8,128)(2,1)S(1)}, u32[]{:S(2)}, u32[]{:S(2)}) collective-permute-start(bf16[192,256]{1,0:T(8,128)(2,1)S(1)} %get-tuple-element.379), channel_id=1, source_target_pairs={{0,4},{4,8},{8,12},{12,16},{16,20},{20,24},{24,28},{1,5},{5,9},{9,... | collective-permute-start | bytes 294920 | tf_op jit(solution)/shard_map/while/body/eval_jaxpr/ppermute | solution.py:14
  33.4 9.6 %collective-permute-start.1 = (bf16[192,256]{1,0:T(8,128)(2,1)S(1)}, bf16[192,256]{1,0:T(8,128)(2,1)S(1)}, u32[]{:S(2)}, u32[]{:S(2)}) collective-permute-start(bf16[192,256]{1,0:T(8,128)(2,1)S(1)} %get-tuple-element.380), channel_id=1, source_target_pairs={{0,4},{4,8},{8,12},{12,16},{16,20},{20,24},{24,28},{1,5},{5,9},{9,... | collective-permute-start | bytes 294920 | tf_op jit(solution)/shard_map/while/body/eval_jaxpr/ppermute | solution.py:14
  35.5 6.7 %collective-permute-start = (bf16[192,256]{1,0:T(8,128)(2,1)S(1)}, bf16[192,256]{1,0:T(8,128)(2,1)S(1)}, u32[]{:S(2)}, u32[]{:S(2)}) collective-permute-start(bf16[192,256]{1,0:T(8,128)(2,1)S(1)} %get-tuple-element.379), channel_id=1, source_target_pairs={{0,4},{4,8},{8,12},{12,16},{16,20},{20,24},{24,28},{1,5},{5,9},{9,... | collective-permute-start | bytes 294920 | tf_op jit(solution)/shard_map/while/body/eval_jaxpr/ppermute | solution.py:14
  43.8 10.1 %collective-permute-start.1 = (bf16[192,256]{1,0:T(8,128)(2,1)S(1)}, bf16[192,256]{1,0:T(8,128)(2,1)S(1)}, u32[]{:S(2)}, u32[]{:S(2)}) collective-permute-start(bf16[192,256]{1,0:T(8,128)(2,1)S(1)} %get-tuple-element.380), channel_id=1, source_target_pairs={{0,4},{4,8},{8,12},{12,16},{16,20},{20,24},{24,28},{1,5},{5,9},{9,... | collective-permute-start | bytes 294920 | tf_op jit(solution)/shard_map/while/body/eval_jaxpr/ppermute | solution.py:14
  46.9 6.3 %collective-permute-start = (bf16[192,256]{1,0:T(8,128)(2,1)S(1)}, bf16[192,256]{1,0:T(8,128)(2,1)S(1)}, u32[]{:S(2)}, u32[]{:S(2)}) collective-permute-start(bf16[192,256]{1,0:T(8,128)(2,1)S(1)} %get-tuple-element.379), channel_id=1, source_target_pairs={{0,4},{4,8},{8,12},{12,16},{16,20},{20,24},{24,28},{1,5},{5,9},{9,... | collective-permute-start | bytes 294920 | tf_op jit(solution)/shard_map/while/body/eval_jaxpr/ppermute | solution.py:14
Sparse Core Ops, SparseCore 0:
  66.6 41.2 reduce-scatter.1
where the time goes:
time: 117 us; the launch traced here: 115 us
  waiting for transfers between devices  54.2 us (46%)
  starting transfers between devices  23.1 us (20%)
  matrix products  16.4 us (14%)
  between operations  13.5 us (12%)
  local copies, waits for them, and re-layouts  4.06 us (3%)
  other arithmetic  2.87 us (2%)
    reduce_scatter x1, waiting for transfers between devices, per_device(): lax.psum_scatter(jnp.dot(context, output_weight, preferred_element_type=j...  41.4 us
    ppermute x8, starting transfers between devices, shifted(): return lax.ppermute(block, axis, route)  23.1 us
    ppermute x8, waiting for transfers between devices, shifted(): return lax.ppermute(block, axis, route)  12.8 us
    dot_general x1, matrix products, per_device(): jnp.dot(context, output_weight, preferred_element_type=jnp.float32)  10.9 us
    dot_general x5, matrix products, attend_block(): jnp.einsum('kgtu,ukd->kgtd', exponent.astype(jnp.bfloat16), value_block.r...  3.44 us
  transfers between devices with their start and end apart: 9, of which 5 were waited for; matrix products, arithmetic and copies ran while one was open for 3% of the time, Pallas kernels for 0%

commit v1 on v0

v1 whole, which is shorter than its diff:
```python
import functools

import jax
import jax.numpy as jnp
from jax import lax
from jax.experimental import pallas as pl
from jax.experimental.pallas import tpu as pltpu
from jax.sharding import PartitionSpec as P

HEADS = 32
KV = 8
HD = 128
GROUP = HEADS // KV
MESH = pl.DeviceIdType.MESH
LOG2E = 1.4426950408889634
SCALE = LOG2E / HD**0.5
MASKED = -1e30
CHUNKS = 16


def kernel(
    n_seq, n_tp, reach,
    q_hbm, k_hbm, v_hbm, doc_ref, w_hbm, out_ref,
    q_all, q, kv, w, m, l, acc, ctx, res, d2d_src, d2d_dst, y_src, y_dst, fin,
    q_sem, own_sem, w_sem, recv_sem, zsend_sem, xsend_sem,
    d2d_send, d2d_recv, y_send, y_recv,
):
    s = lax.axis_index("seq")
    t = lax.axis_index("tp")
    tokens = q_hbm.shape[0]
    heads_kv = k_hbm.shape[1] // HD
    pieces = 2 * heads_kv
    chips = n_tp // 2
    rows = tokens // n_tp
    width = out_ref.shape[1] // CHUNKS
    odd = s % 2
    partner = s + 1 - 2 * odd
    core = t % 2
    chip = t // 2
    sibling = t + 1 - 2 * core

    def q_copy():
        return pltpu.make_async_copy(q_hbm, q_all, q_sem)

    def own_copy(c):
        src = k_hbm if c % 2 == 0 else v_hbm
        return pltpu.make_async_copy(
            src.at[:, pl.ds((c // 2) * HD, HD)], kv.at[0, c], own_sem.at[c]
        )

    def w_copy(j):
        cols = pl.ds(pl.multiple_of(j * width, width), width)
        return pltpu.make_async_copy(w_hbm.at[:, cols], w.at[:, cols], w_sem.at[j])

    for c in range(pieces):
        own_copy(c).start()
    q_copy().start()

    barrier = pltpu.get_barrier_semaphore()

    def greet(seq_index, tp_index):
        pl.semaphore_signal(
            barrier, inc=1, device_id=(seq_index, tp_index), device_id_type=MESH
        )

    greet(partner, t)
    greet(s, sibling)
    for step in range(1, chips):
        greet(s, ((chip + step) % chips) * 2 + core)

    @pl.when(s >= 2)
    def _():
        greet(s - 2, t)

    @pl.when(s + 2 < n_seq)
    def _():
        greet(s + 2, t)

    for j in range(CHUNKS):
        w_copy(j).start()

    along = (s >= 2).astype(jnp.int32) + (s + 2 < n_seq).astype(jnp.int32)
    pl.semaphore_wait(barrier, chips + 1 + along)

    def z_copy(d, c):
        return pltpu.make_async_remote_copy(
            src_ref=kv.at[d, c], dst_ref=kv.at[d + 2, c],
            send_sem=zsend_sem.at[d, c], recv_sem=recv_sem.at[d + 2, c],
            device_id=(s + 2, t), device_id_type=MESH,
        )

    def x_copy(d, to, c):
        return pltpu.make_async_remote_copy(
            src_ref=kv.at[d, c], dst_ref=kv.at[to, c],
            send_sem=xsend_sem.at[d, c], recv_sem=recv_sem.at[to, c],
            device_id=(partner, t), device_id_type=MESH,
        )

    def arrival(d, c):
        return pltpu.make_async_remote_copy(
            src_ref=kv.at[d, c], dst_ref=kv.at[d, c],
            send_sem=xsend_sem.at[d, c], recv_sem=recv_sem.at[d, c],
            device_id=(partner, t), device_id_type=MESH,
        )

    def for_sends(d, act):
        if d + 2 <= reach:
            @pl.when((s >= d) & (s + 2 < n_seq))
            def _():
                act(lambda c: z_copy(d, c))
        if d + 1 <= reach:
            @pl.when((s >= d) & (odd == 0))
            def _():
                act(lambda c: x_copy(d, d + 1, c))
        if d >= 2:
            @pl.when((s >= d) & (odd == 1))
            def _():
                act(lambda c: x_copy(d, d - 1, c))

    for c in range(pieces):
        own_copy(c).wait()
        for_sends(0, lambda copy, c=c: copy(c).start())

    q_copy().wait()
    for h in range(heads_kv * GROUP):
        q[h // GROUP, pl.ds((h % GROUP) * tokens, tokens), :] = q_all[:, h * HD:(h + 1) * HD]

    row_of = lax.broadcasted_iota(jnp.int32, (tokens, tokens), 0)
    col_of = lax.broadcasted_iota(jnp.int32, (tokens, tokens), 1)
    own_doc = doc_ref[pl.ds(s, 1), :].astype(jnp.float32)
    doc_col = jnp.sum(jnp.where(row_of == col_of, own_doc, 0.0), axis=1, keepdims=True)

    def attend(d, g):
        key_doc = doc_ref[pl.ds(s - d, 1), :].astype(jnp.float32)
        allowed = key_doc == doc_col
        if d == 0:
            allowed = allowed & (col_of <= row_of)
        bias = jnp.where(allowed, 0.0, MASKED)
        scores = lax.dot_general(
            q[g], kv[d, 2 * g], (((1,), (1,)), ((), ())), preferred_element_type=jnp.float32
        )
        scores = scores.reshape(GROUP, tokens, tokens) * SCALE + bias[None]
        scores = scores.reshape(GROUP * tokens, tokens)
        top = jnp.max(scores, axis=1, keepdims=True)
        if d == 0:
            new_m = top
        else:
            old_m = m[g]
            new_m = jnp.maximum(old_m, top)
        p = jnp.exp2(scores - new_m)
        total = jnp.sum(p, axis=1, keepdims=True)
        if d > 0:
            arrival(d, 2 * g + 1).wait_recv()
            if d % 2 == 0:
                for_sends(d, lambda copy: copy(2 * g + 1).start())
        added = jnp.dot(
            p.astype(jnp.bfloat16), kv[d, 2 * g + 1], preferred_element_type=jnp.float32
        )
        m[g] = new_m
        if d == 0:
            l[g] = total
            acc[g] = added
        else:
            rescale = jnp.exp2(old_m - new_m)
            l[g] = l[g] * rescale + total
            acc[g] = acc[g] * rescale + added

    order = [0]
    for d in range(2, reach + 1, 2):
        order += [d, d - 1]
    for d in order:
        @pl.when(s >= d)
        def _(d=d):
            @pl.loop(0, heads_kv)
            def _(g):
                if d > 0:
                    arrival(d, 2 * g).wait_recv()
                    if d % 2 == 0:
                        for_sends(d, lambda copy: copy(2 * g).start())
                attend(d, g)

    for h in range(heads_kv * GROUP):
        g, part = h // GROUP, pl.ds((h % GROUP) * tokens, tokens)
        ctx[:, h * HD:(h + 1) * HD] = (acc[g, part, :] / l[g, part, :]).astype(jnp.bfloat16)

    def d2d_copy(j):
        return pltpu.make_async_remote_copy(
            src_ref=d2d_src.at[j], dst_ref=d2d_dst.at[j],
            send_sem=d2d_send.at[j], recv_sem=d2d_recv.at[j],
            device_id=(s, sibling), device_id_type=MESH,
        )

    def y_copy(j, step):
        return pltpu.make_async_remote_copy(
            src_ref=y_src.at[j, step - 1], dst_ref=y_dst.at[j, step - 1],
            send_sem=y_send.at[j, step - 1], recv_sem=y_recv.at[j, step - 1],
            device_id=(s, ((chip + step) % chips) * 2 + core), device_id_type=MESH,
        )

    def rows_of(j, owner):
        return res[j % 2, pl.ds(pl.multiple_of(owner * rows, 8), rows), :]

    def project(j):
        w_copy(j).wait()
        cols = pl.ds(pl.multiple_of(j * width, width), width)
        res[j % 2] = jnp.dot(ctx[...], w[:, cols], preferred_element_type=jnp.float32)
        for y in range(chips):
            d2d_src[j, y] = rows_of(j, y * 2 + 1 - core).astype(jnp.bfloat16)
        d2d_copy(j).start()

    def pair_up(j):
        d2d_copy(j).wait_recv()
        for step in range(1, chips):
            other = (chip + step) % chips
            pair = rows_of(j, other * 2 + core) + d2d_dst[j, other].astype(jnp.float32)
            y_src[j, step - 1] = pair.astype(jnp.bfloat16)
            y_copy(j, step).start()
        fin[j] = rows_of(j, t) + d2d_dst[j, chip].astype(jnp.float32)

    project(0)

    @pl.loop(1, CHUNKS)
    def _(j):
        project(j)
        pair_up(j - 1)

    pair_up(CHUNKS - 1)

    @pl.loop(0, CHUNKS)
    def _(j):
        total = fin[j]
        for step in range(1, chips):
            y_copy(j, step).wait_recv()
            total = total + y_dst[j, step - 1].astype(jnp.float32)
        cols = pl.ds(pl.multiple_of(j * width, width), width)
        out_ref[:, cols] = total.astype(out_ref.dtype)

    for d in range(0, reach + 1, 2):
        def drain(copy):
            for c in range(pieces):
                copy(c).wait_send()
        for_sends(d, drain)

    @pl.loop(0, CHUNKS)
    def _(j):
        d2d_copy(j).wait_send()
        for step in range(1, chips):
            y_copy(j, step).wait_send()


def solution(mesh):
    n_seq, n_tp = mesh.shape["seq"], mesh.shape["tp"]
    reach = min(12, n_seq // 2)
    chips = n_tp // 2

    def per_device(query_rows, key_rows, value_rows, document_ids, output_weight):
        tokens, q_width = query_rows.shape
        heads_kv = key_rows.shape[1] // HD
        depth, model = output_weight.shape
        rows, width = tokens // n_tp, model // CHUNKS
        bf16, f32 = jnp.bfloat16, jnp.float32
        dma = pltpu.SemaphoreType.DMA
        docs = document_ids.reshape(n_seq, tokens)
        any_space = pl.BlockSpec(memory_space=pl.ANY)
        in_vmem = pl.BlockSpec(memory_space=pltpu.VMEM)
        return pl.pallas_call(
            functools.partial(kernel, n_seq, n_tp, reach),
            out_shape=jax.ShapeDtypeStruct((rows, model), bf16),
            in_specs=[any_space, any_space, any_space, in_vmem, any_space],
            out_specs=in_vmem,
            scratch_shapes=[
                pltpu.VMEM((tokens, q_width), bf16),
                pltpu.VMEM((heads_kv, GROUP * tokens, HD), bf16),
                pltpu.VMEM((reach + 1, 2 * heads_kv, tokens, HD), bf16),
                pltpu.VMEM((depth, model), bf16),
                pltpu.VMEM((heads_kv, GROUP * tokens, 1), f32),
                pltpu.VMEM((heads_kv, GROUP * tokens, 1), f32),
                pltpu.VMEM((heads_kv, GROUP * tokens, HD), f32),
                pltpu.VMEM((tokens, q_width), bf16),
                pltpu.VMEM((2, tokens, width), f32),
                pltpu.VMEM((CHUNKS, chips, rows, width), bf16),
                pltpu.VMEM((CHUNKS, chips, rows, width), bf16),
                pltpu.VMEM((CHUNKS, chips - 1, rows, width), bf16),
                pltpu.VMEM((CHUNKS, chips - 1, rows, width), bf16),
                pltpu.VMEM((CHUNKS, rows, width), f32),
                dma, dma((2 * heads_kv,)), dma((CHUNKS,)),
                dma((reach + 1, 2 * heads_kv)),
                dma((reach + 1, 2 * heads_kv)),
                dma((reach + 1, 2 * heads_kv)),
                dma((CHUNKS,)), dma((CHUNKS,)),
                dma((CHUNKS, chips - 1)), dma((CHUNKS, chips - 1)),
            ],
            compiler_params=pltpu.CompilerParams(
                collective_id=0, has_side_effects=True, vmem_limit_bytes=60 * 1024 * 1024
            ),
        )(query_rows, key_rows, value_rows, docs, output_weight)

    in_specs = (P("seq", "tp"), P("seq", "tp"), P("seq", "tp"), P(), P("tp", None))
    return jax.shard_map(
        per_device, mesh=mesh, in_specs=in_specs, out_specs=P(("seq", "tp"), None),
        check_vma=False,
    )
```

time: 117 us -> 49.4 us (0.42); the launches traced: 115 us -> 49.2 us
  waiting for transfers between devices: 54.2 us -> 0 us
  Pallas kernels: 0 us -> 45.8 us
  starting transfers between devices: 23.1 us -> 0 us
  matrix products: 16.4 us -> 0 us
  between operations: 13.5 us -> 0.01 us
  other arithmetic: 2.87 us -> 0 us
    pallas_call x0 -> x1, Pallas kernels: none -> 45.8 us  [per_device(): pl.pallas_call(functools.partial(kernel, n_seq, n_tp, reach), out_shape=j...]
    reduce_scatter x1 -> x0, waiting for transfers between devices: 41.4 us -> none  [per_device(): lax.psum_scatter(jnp.dot(context, output_weight, preferred_element_type=j...]
    ppermute x8 -> x0, starting transfers between devices: 23.1 us -> none  [shifted(): return lax.ppermute(block, axis, route)]
    dot_general x11 -> x0, matrix products: 16.4 us -> none  [the longest x1 10.9 us: per_device(): jnp.dot(context, output_weight, preferred_element_type=jnp.float32)]
    ppermute x8 -> x0, waiting for transfers between devices: 12.8 us -> none  [shifted(): return lax.ppermute(block, axis, route)]
    reduce_sum x5 -> x0, other arithmetic: 1.31 us -> none  [attend_block(): new_sum = running_sum * rescale + jnp.sum(exponent, axis=-1)]
  transfers between devices with their start and end apart: 9 -> 0, of which waited for: 5 -> 0; matrix products, arithmetic and copies ran while one was open for 3% -> 0% of each run, Pallas kernels for 0% -> 0%
where the time goes in v1:
time: 49.4 us; the launch traced here: 49.2 us
  Pallas kernels  45.8 us (93%)
  local copies, waits for them, and re-layouts  3.43 us (7%)
    pallas_call x1, Pallas kernels, per_device(): pl.pallas_call(functools.partial(kernel, n_seq, n_tp, reach), out_shape=j...  45.8 us
    unnamed x1, local copies, waits for them, and re-layouts  2.06 us
    reshape x1, local copies, waits for them, and re-layouts, per_device(): docs = document_ids.reshape(n_seq, tokens)  1.36 us

profile of v1, /device:TPU:17, one launch (start us, length us, event | category | flops | bytes accessed | tf_op | source)
XLA Modules:
  0.0 49.2 jit_solution(4584758706748085880)
XLA Ops:
  0.0 1.4 %reshape.3.doc_ref = s32[8,192]{1,0:T(8,128)} reshape(s32[1536]{0:T(1024)} %param.8) | data formatting | bytes 12288 | tf_op jit(solution)/shard_map/reshape | solution.py:263
  1.4 45.8 %shard_map.55 = bf16[48,8192]{1,0:T(8,128)(2,1)} custom-call(bf16[192,1024]{1,0:T(8,128)(2,1)} %q_hbm.1, bf16[192,256]{1,0:T(8,128)(2,1)} %k_hbm.1, bf16[192,256]{1,0:T(8,128)(2,1)} %v_hbm.1, s32[8,192]{1,0:T(8,128)} %reshape.3.doc_ref, bf16[1024,8192]{1,0:T(8,128)(2,1)} %w_hbm.1), custom_call_target="tpu_custom_call" | custom-call | tf_op jit(solution)/shard_map/pallas_call | solution.py:266
  47.1 2.1 %copy.7 = bf16[48,8192]{1,0:T(8,128)(2,1)} copy(bf16[48,8192]{1,0:T(8,128)(2,1)} %shard_map.55) | data formatting | bytes 1572864

commit v2 on v1

--- a/solution.py
+++ b/solution.py
@@ -1,4 +1,5 @@
 import functools
+import math
 
 import jax
 import jax.numpy as jnp
@@ -20,9 +21,9 @@
 
 def kernel(
     n_seq, n_tp, reach,
-    q_hbm, k_hbm, v_hbm, doc_ref, w_hbm, out_ref,
-    q_all, q, kv, w, m, l, acc, ctx, res, d2d_src, d2d_dst, y_src, y_dst, fin,
-    q_sem, own_sem, w_sem, recv_sem, zsend_sem, xsend_sem,
+    q_hbm, k_hbm, v_hbm, doc_hbm, w_hbm, out_ref,
+    q_all, q, kv, w, docs, q_doc, q_pos, key_docs, m, l, acc, ctx, res, d2d_src, d2d_dst, y_src, y_dst, fin,
+    q_sem, doc_sem, own_sem, w_sem, recv_sem, zsend_sem, xsend_sem,
     d2d_send, d2d_recv, y_send, y_recv,
 ):
     s = lax.axis_index("seq")
@@ -38,9 +39,13 @@
     core = t % 2
     chip = t // 2
     sibling = t + 1 - 2 * core
+    tile = math.gcd(GROUP * tokens, 256)
 
     def q_copy():
         return pltpu.make_async_copy(q_hbm, q_all, q_sem)
+
+    def doc_copy():
+        return pltpu.make_async_copy(doc_hbm, docs, doc_sem)
 
     def own_copy(c):
         src = k_hbm if c % 2 == 0 else v_hbm
@@ -55,6 +60,7 @@
     for c in range(pieces):
         own_copy(c).start()
     q_copy().start()
+    doc_copy().start()
 
     barrier = pltpu.get_barrier_semaphore()
 
@@ -125,45 +131,73 @@
     for h in range(heads_kv * GROUP):
         q[h // GROUP, pl.ds((h % GROUP) * tokens, tokens), :] = q_all[:, h * HD:(h + 1) * HD]
 
+    doc_copy().wait()
+    lanes = 128
+    span = (tokens + lanes - math.gcd(tokens, lanes) + lanes - 1) // lanes
+    key_of = lax.broadcasted_iota(jnp.int32, (tokens, span * lanes), 0)
+    lane_of = lax.broadcasted_iota(jnp.int32, (tokens, span * lanes), 1)
+
+    def docs_down(block):
+        first = block * tokens
+        top_row, shift = first // lanes, first % lanes
+        ids = jnp.concatenate(
+            [
+                docs[pl.ds(jnp.minimum(top_row + i, docs.shape[0] - 1), 1), :]
+                for i in range(span)
+            ],
+            axis=1,
+        ).astype(jnp.float32)
+        return jnp.sum(jnp.where(lane_of == key_of + shift, ids, 0.0), axis=1, keepdims=True)
+
     row_of = lax.broadcasted_iota(jnp.int32, (tokens, tokens), 0)
     col_of = lax.broadcasted_iota(jnp.int32, (tokens, tokens), 1)
-    own_doc = doc_ref[pl.ds(s, 1), :].astype(jnp.float32)
-    doc_col = jnp.sum(jnp.where(row_of == col_of, own_doc, 0.0), axis=1, keepdims=True)
+    own_row = jnp.sum(
+        jnp.where(row_of == col_of, docs_down(s), 0.0), axis=0, keepdims=True
+    )
+    q_doc[...] = jnp.concatenate([own_row] * GROUP, axis=1)
+    q_pos[...] = jnp.concatenate([col_of[:1]] * GROUP, axis=1)
+    tiles = [pl.ds(i * tile, tile) for i in range(GROUP * tokens // tile)]
 
     def attend(d, g):
-        key_doc = doc_ref[pl.ds(s - d, 1), :].astype(jnp.float32)
-        allowed = key_doc == doc_col
-        if d == 0:
-            allowed = allowed & (col_of <= row_of)
-        bias = jnp.where(allowed, 0.0, MASKED)
-        scores = lax.dot_general(
-            q[g], kv[d, 2 * g], (((1,), (1,)), ((), ())), preferred_element_type=jnp.float32
-        )
-        scores = scores.reshape(GROUP, tokens, tokens) * SCALE + bias[None]
-        scores = scores.reshape(GROUP * tokens, tokens)
-        top = jnp.max(scores, axis=1, keepdims=True)
-        if d == 0:
-            new_m = top
-        else:
-            old_m = m[g]
-            new_m = jnp.maximum(old_m, top)
-        p = jnp.exp2(scores - new_m)
-        total = jnp.sum(p, axis=1, keepdims=True)
+        key_doc = key_docs[...]
+        probs = []
+        for cols in tiles:
+            scores = lax.dot_general(
+                kv[d, 2 * g], q[g, cols, :], (((1,), (1,)), ((), ())),
+                preferred_element_type=jnp.float32,
+            )
+            allowed = key_doc == q_doc[:, cols]
+            if d == 0:
+                key_pos = lax.broadcasted_iota(jnp.int32, (tokens, tile), 0)
+                allowed = allowed & (key_pos <= q_pos[:, cols])
+            scores = jnp.where(allowed, scores * SCALE, MASKED)
+            top = jnp.max(scores, axis=0, keepdims=True)
+            if d == 0:
+                p = jnp.exp2(scores - top)
+                l[g, :, cols] = jnp.sum(p, axis=0, keepdims=True)
+                m[g, :, cols] = top
+                rescale = None
+            else:
+                old_m = m[g, :, cols]
+                new_m = jnp.maximum(old_m, top)
+                p = jnp.exp2(scores - new_m)
+                rescale = jnp.exp2(old_m - new_m)
+                l[g, :, cols] = l[g, :, cols] * rescale + jnp.sum(p, axis=0, keepdims=True)
+                m[g, :, cols] = new_m
+            probs.append((p.astype(jnp.bfloat16), rescale))
         if d > 0:
             arrival(d, 2 * g + 1).wait_recv()
             if d % 2 == 0:
                 for_sends(d, lambda copy: copy(2 * g + 1).start())
-        added = jnp.dot(
-            p.astype(jnp.bfloat16), kv[d, 2 * g + 1], preferred_element_type=jnp.float32
-        )
-        m[g] = new_m
-        if d == 0:
-            l[g] = total
-            acc[g] = added
-        else:
-            rescale = jnp.exp2(old_m - new_m)
-            l[g] = l[g] * rescale + total
-            acc[g] = acc[g] * rescale + added
+        for cols, (p, rescale) in zip(tiles, probs):
+            added = lax.dot_general(
+                kv[d, 2 * g + 1], p, (((0,), (0,)), ((), ())),
+                preferred_element_type=jnp.float32,
+            )
+            if d == 0:
+                acc[g, :, cols] = added
+            else:
+                acc[g, :, cols] = acc[g, :, cols] * rescale + added
 
     order = [0]
     for d in range(2, reach + 1, 2):
@@ -171,6 +205,8 @@
     for d in order:
         @pl.when(s >= d)
         def _(d=d):
+            key_docs[...] = docs_down(s - d)
+
             @pl.loop(0, heads_kv)
             def _(g):
                 if d > 0:
@@ -179,9 +215,11 @@
                         for_sends(d, lambda copy: copy(2 * g).start())
                 attend(d, g)
 
-    for h in range(heads_kv * GROUP):
-        g, part = h // GROUP, pl.ds((h % GROUP) * tokens, tokens)
-        ctx[:, h * HD:(h + 1) * HD] = (acc[g, part, :] / l[g, part, :]).astype(jnp.bfloat16)
+    for g in range(heads_kv):
+        mixed = jnp.transpose(acc[g] / l[g]).astype(jnp.bfloat16)
+        for i in range(GROUP):
+            h = g * GROUP + i
+            ctx[:, h * HD:(h + 1) * HD] = mixed[i * tokens:(i + 1) * tokens, :]
 
     def d2d_copy(j):
         return pltpu.make_async_remote_copy(
@@ -260,22 +298,26 @@
         rows, width = tokens // n_tp, model // CHUNKS
         bf16, f32 = jnp.bfloat16, jnp.float32
         dma = pltpu.SemaphoreType.DMA
-        docs = document_ids.reshape(n_seq, tokens)
+        docs = document_ids.reshape(-1, 128)
         any_space = pl.BlockSpec(memory_space=pl.ANY)
         in_vmem = pl.BlockSpec(memory_space=pltpu.VMEM)
         return pl.pallas_call(
             functools.partial(kernel, n_seq, n_tp, reach),
             out_shape=jax.ShapeDtypeStruct((rows, model), bf16),
-            in_specs=[any_space, any_space, any_space, in_vmem, any_space],
+            in_specs=[any_space, any_space, any_space, any_space, any_space],
             out_specs=in_vmem,
             scratch_shapes=[
                 pltpu.VMEM((tokens, q_width), bf16),
                 pltpu.VMEM((heads_kv, GROUP * tokens, HD), bf16),
                 pltpu.VMEM((reach + 1, 2 * heads_kv, tokens, HD), bf16),
                 pltpu.VMEM((depth, model), bf16),
-                pltpu.VMEM((heads_kv, GROUP * tokens, 1), f32),
-                pltpu.VMEM((heads_kv, GROUP * tokens, 1), f32),
-                pltpu.VMEM((heads_kv, GROUP * tokens, HD), f32),
+                pltpu.VMEM(docs.shape, jnp.int32),
+                pltpu.VMEM((1, GROUP * tokens), f32),
+                pltpu.VMEM((1, GROUP * tokens), jnp.int32),
+                pltpu.VMEM((tokens, 1), f32),
+                pltpu.VMEM((heads_kv, 1, GROUP * tokens), f32),
+                pltpu.VMEM((heads_kv, 1, GROUP * tokens), f32),
+                pltpu.VMEM((heads_kv, HD, GROUP * tokens), f32),
                 pltpu.VMEM((tokens, q_width), bf16),
                 pltpu.VMEM((2, tokens, width), f32),
                 pltpu.VMEM((CHUNKS, chips, rows, width), bf16),
@@ -283,7 +325,7 @@
                 pltpu.VMEM((CHUNKS, chips - 1, rows, width), bf16),
                 pltpu.VMEM((CHUNKS, chips - 1, rows, width), bf16),
                 pltpu.VMEM((CHUNKS, rows, width), f32),
-                dma, dma((2 * heads_kv,)), dma((CHUNKS,)),
+                dma, dma, dma((2 * heads_kv,)), dma((CHUNKS,)),
                 dma((reach + 1, 2 * heads_kv)),
                 dma((reach + 1, 2 * heads_kv)),
                 dma((reach + 1, 2 * heads_kv)),

time: 49.4 us -> 41 us (0.83)
  Pallas kernels: 45.8 us -> 38.8 us
  local copies, waits for them, and re-layouts: 3.43 us -> 2.06 us
    pallas_call x1, Pallas kernels: 45.8 us -> 38.8 us  [per_device(): pl.pallas_call(functools.partial(kernel, n_seq, n_tp, reach), out_shape=j...]
    reshape x1 -> x0, local copies, waits for them, and re-layouts: 1.36 us -> none  [per_device(): docs = document_ids.reshape(n_seq, tokens)]
where the time goes in v2:
time: 41 us; the launch traced here: 40.9 us
  Pallas kernels  38.8 us (95%)
  local copies, waits for them, and re-layouts  2.06 us (5%)
    pallas_call x1, Pallas kernels, per_device(): pl.pallas_call(functools.partial(kernel, n_seq, n_tp, reach), out_shape=j...  38.8 us
    unnamed x1, local copies, waits for them, and re-layouts  2.06 us

profile of v2, /device:TPU:17, one launch (start us, length us, event | category | flops | bytes accessed | tf_op | source)
XLA Modules:
  0.0 40.9 jit_solution(1098793442862915200)
XLA Ops:
  0.0 38.8 %shard_map.55 = bf16[48,8192]{1,0:T(8,128)(2,1)} custom-call(bf16[192,1024]{1,0:T(8,128)(2,1)} %q_hbm.1, bf16[192,256]{1,0:T(8,128)(2,1)} %k_hbm.1, bf16[192,256]{1,0:T(8,128)(2,1)} %v_hbm.1, s32[12,128]{1,0:T(8,128)} %bitcast.1, bf16[1024,8192]{1,0:T(8,128)(2,1)} %w_hbm.1), custom_call_target="tpu_custom_call" | custom-call | tf_op jit(solution)/shard_map/pallas_call | solution.py:304
  38.8 2.1 %copy.7 = bf16[48,8192]{1,0:T(8,128)(2,1)} copy(bf16[48,8192]{1,0:T(8,128)(2,1)} %shard_map.55) | data formatting | bytes 1572864

commit v3 on v2

--- a/solution.py
+++ b/solution.py
@@ -30,7 +30,8 @@
     t = lax.axis_index("tp")
     tokens = q_hbm.shape[0]
     heads_kv = k_hbm.shape[1] // HD
-    pieces = 2 * heads_kv
+    pieces = 4 * heads_kv
+    half = tokens // 2
     chips = n_tp // 2
     rows = tokens // n_tp
     width = out_ref.shape[1] // CHUNKS
@@ -48,9 +49,10 @@
         return pltpu.make_async_copy(doc_hbm, docs, doc_sem)
 
     def own_copy(c):
-        src = k_hbm if c % 2 == 0 else v_hbm
+        src = k_hbm if c % 4 < 2 else v_hbm
         return pltpu.make_async_copy(
-            src.at[:, pl.ds((c // 2) * HD, HD)], kv.at[0, c], own_sem.at[c]
+            src.at[pl.ds((c % 2) * half, half), pl.ds((c // 4) * HD, HD)],
+            kv.at[0, c], own_sem.at[c],
         )
 
     def w_copy(j):
@@ -123,6 +125,11 @@
             def _():
                 act(lambda c: x_copy(d, d - 1, c))
 
+    def take(d, c):
+        arrival(d, c).wait_recv()
+        if d % 2 == 0:
+            for_sends(d, lambda copy: copy(c).start())
+
     for c in range(pieces):
         own_copy(c).wait()
         for_sends(0, lambda copy, c=c: copy(c).start())
@@ -160,10 +167,11 @@
 
     def attend(d, g):
         key_doc = key_docs[...]
+        keys = kv[d, pl.ds(4 * g, 2)].reshape(tokens, HD)
         probs = []
         for cols in tiles:
             scores = lax.dot_general(
-                kv[d, 2 * g], q[g, cols, :], (((1,), (1,)), ((), ())),
+                keys, q[g, cols, :], (((1,), (1,)), ((), ())),
                 preferred_element_type=jnp.float32,
             )
             allowed = key_doc == q_doc[:, cols]
@@ -186,12 +194,12 @@
                 m[g, :, cols] = new_m
             probs.append((p.astype(jnp.bfloat16), rescale))
         if d > 0:
-            arrival(d, 2 * g + 1).wait_recv()
-            if d % 2 == 0:
-                for_sends(d, lambda copy: copy(2 * g + 1).start())
+            take(d, 4 * g + 2)
+            take(d, 4 * g + 3)
+        values = kv[d, pl.ds(4 * g + 2, 2)].reshape(tokens, HD)
         for cols, (p, rescale) in zip(tiles, probs):
             added = lax.dot_general(
-                kv[d, 2 * g + 1], p, (((0,), (0,)), ((), ())),
+                values, p, (((0,), (0,)), ((), ())),
                 preferred_element_type=jnp.float32,
             )
             if d == 0:
@@ -210,9 +218,8 @@
             @pl.loop(0, heads_kv)
             def _(g):
                 if d > 0:
-                    arrival(d, 2 * g).wait_recv()
-                    if d % 2 == 0:
-                        for_sends(d, lambda copy: copy(2 * g).start())
+                    take(d, 4 * g)
+                    take(d, 4 * g + 1)
                 attend(d, g)
 
     for g in range(heads_kv):
@@ -299,17 +306,17 @@
         bf16, f32 = jnp.bfloat16, jnp.float32
         dma = pltpu.SemaphoreType.DMA
         docs = document_ids.reshape(-1, 128)
-        any_space = pl.BlockSpec(memory_space=pl.ANY)
+        in_hbm = pl.BlockSpec(memory_space=pltpu.HBM)
         in_vmem = pl.BlockSpec(memory_space=pltpu.VMEM)
         return pl.pallas_call(
             functools.partial(kernel, n_seq, n_tp, reach),
-            out_shape=jax.ShapeDtypeStruct((rows, model), bf16),
-            in_specs=[any_space, any_space, any_space, any_space, any_space],
+            out_shape=pltpu.VMEM((rows, model), bf16),
+            in_specs=[in_hbm] * 5,
             out_specs=in_vmem,
             scratch_shapes=[
                 pltpu.VMEM((tokens, q_width), bf16),
                 pltpu.VMEM((heads_kv, GROUP * tokens, HD), bf16),
-                pltpu.VMEM((reach + 1, 2 * heads_kv, tokens, HD), bf16),
+                pltpu.VMEM((reach + 1, 4 * heads_kv, tokens // 2, HD), bf16),
                 pltpu.VMEM((depth, model), bf16),
                 pltpu.VMEM(docs.shape, jnp.int32),
                 pltpu.VMEM((1, GROUP * tokens), f32),
@@ -325,10 +332,10 @@
                 pltpu.VMEM((CHUNKS, chips - 1, rows, width), bf16),
                 pltpu.VMEM((CHUNKS, chips - 1, rows, width), bf16),
                 pltpu.VMEM((CHUNKS, rows, width), f32),
-                dma, dma, dma((2 * heads_kv,)), dma((CHUNKS,)),
-                dma((reach + 1, 2 * heads_kv)),
-                dma((reach + 1, 2 * heads_kv)),
-                dma((reach + 1, 2 * heads_kv)),
+                dma, dma, dma((4 * heads_kv,)), dma((CHUNKS,)),
+                dma((reach + 1, 4 * heads_kv)),
+                dma((reach + 1, 4 * heads_kv)),
+                dma((reach + 1, 4 * heads_kv)),
                 dma((CHUNKS,)), dma((CHUNKS,)),
                 dma((CHUNKS, chips - 1)), dma((CHUNKS, chips - 1)),
             ],

time: 41 us -> 39.3 us (0.959)
  local copies, waits for them, and re-layouts: 2.06 us -> 0.88 us
  Pallas kernels: 38.8 us -> 38.3 us
    unnamed x1, local copies, waits for them, and re-layouts: 2.06 us -> 0.88 us
    pallas_call x1, Pallas kernels: 38.8 us -> 38.3 us  [per_device(): pl.pallas_call(functools.partial(kernel, n_seq, n_tp, reach), out_shape=p...]
where the time goes in v3:
time: 39.3 us; the launch traced here: 39.2 us
  Pallas kernels  38.3 us (97%)
  local copies, waits for them, and re-layouts  0.88 us (2%)
    pallas_call x1, Pallas kernels, per_device(): pl.pallas_call(functools.partial(kernel, n_seq, n_tp, reach), out_shape=p...  38.3 us
    unnamed x1, local copies, waits for them, and re-layouts  0.88 us

profile of v3, /device:TPU:17, one launch (start us, length us, event | category | flops | bytes accessed | tf_op | source)
XLA Modules:
  0.0 39.2 jit_solution(2033900811108975058)
XLA Ops:
  0.0 38.3 %shard_map.55 = bf16[48,8192]{1,0:T(8,128)(2,1)S(1)} custom-call(bf16[192,1024]{1,0:T(8,128)(2,1)} %q_hbm.1, bf16[192,256]{1,0:T(8,128)(2,1)} %k_hbm.1, bf16[192,256]{1,0:T(8,128)(2,1)} %v_hbm.1, s32[12,128]{1,0:T(8,128)} %bitcast.1, bf16[1024,8192]{1,0:T(8,128)(2,1)} %w_hbm.1), custom_call_target="tpu_custom_call" | custom-call | tf_op jit(solution)/shard_map/pallas_call | solution.py:311
  38.3 0.9 %copy.7 = bf16[48,8192]{1,0:T(8,128)(2,1)} copy(bf16[48,8192]{1,0:T(8,128)(2,1)S(1)} %shard_map.55) | data formatting | bytes 1572864

commit v4 on v3

--- a/solution.py
+++ b/solution.py
@@ -32,6 +32,7 @@
     heads_kv = k_hbm.shape[1] // HD
     pieces = 4 * heads_kv
     half = tokens // 2
+    late = pieces // 4
     chips = n_tp // 2
     rows = tokens // n_tp
     width = out_ref.shape[1] // CHUNKS
@@ -112,27 +113,38 @@
         )
 
     def for_sends(d, act):
+        if d % 2 == 1:
+            if d + 2 <= reach:
+                @pl.when((s >= d) & (odd == 0) & (s + 2 < n_seq))
+                def _():
+                    act(lambda c: z_copy(d, c), range(pieces - late, pieces))
+            return
         if d + 2 <= reach:
             @pl.when((s >= d) & (s + 2 < n_seq))
             def _():
-                act(lambda c: z_copy(d, c))
+                act(lambda c: z_copy(d, c), range(pieces))
         if d + 1 <= reach:
             @pl.when((s >= d) & (odd == 0))
             def _():
-                act(lambda c: x_copy(d, d + 1, c))
+                act(lambda c: x_copy(d, d + 1, c), range(pieces))
         if d >= 2:
             @pl.when((s >= d) & (odd == 1))
             def _():
-                act(lambda c: x_copy(d, d - 1, c))
+                act(lambda c: x_copy(d, d - 1, c), range(pieces if d == 2 else pieces - late))
 
     def take(d, c):
         arrival(d, c).wait_recv()
-        if d % 2 == 0:
-            for_sends(d, lambda copy: copy(c).start())
+
+        def pass_on(copy, which):
+            @pl.when((c >= which.start) & (c < which.stop))
+            def _():
+                copy(c).start()
+
+        for_sends(d, pass_on)
 
     for c in range(pieces):
         own_copy(c).wait()
-        for_sends(0, lambda copy, c=c: copy(c).start())
+        for_sends(0, lambda copy, which, c=c: copy(c).start())
 
     q_copy().wait()
     for h in range(heads_kv * GROUP):
@@ -210,19 +222,32 @@
     order = [0]
     for d in range(2, reach + 1, 2):
         order += [d, d - 1]
-    for d in order:
+    def visit(d, g):
+        if d > 0:
+            take(d, 4 * g)
+            take(d, 4 * g + 1)
+        attend(d, g)
+
+    for d in order[:-1]:
         @pl.when(s >= d)
         def _(d=d):
             key_docs[...] = docs_down(s - d)
 
             @pl.loop(0, heads_kv)
             def _(g):
-                if d > 0:
-                    take(d, 4 * g)
-                    take(d, 4 * g + 1)
-                attend(d, g)
+                visit(d, g)
+
+    last = order[-1]
+
+    @pl.when(s >= last)
+    def _():
+        key_docs[...] = docs_down(s - last)
 
     for g in range(heads_kv):
+        @pl.when(s >= last)
+        def _(g=g):
+            visit(last, g)
+
         mixed = jnp.transpose(acc[g] / l[g]).astype(jnp.bfloat16)
         for i in range(GROUP):
             h = g * GROUP + i
@@ -280,9 +305,9 @@
         cols = pl.ds(pl.multiple_of(j * width, width), width)
         out_ref[:, cols] = total.astype(out_ref.dtype)
 
-    for d in range(0, reach + 1, 2):
-        def drain(copy):
-            for c in range(pieces):
+    for d in range(reach + 1):
+        def drain(copy, which):
+            for c in which:
                 copy(c).wait_send()
         for_sends(d, drain)
 

time: 39.3 us -> 39.1 us (level)
  no operation moved by 1% of the time
where the time goes in v4:
time: 39.1 us; the launch traced here: 39 us
  Pallas kernels  38.1 us (97%)
  local copies, waits for them, and re-layouts  0.88 us (2%)
    pallas_call x1, Pallas kernels, per_device(): pl.pallas_call(functools.partial(kernel, n_seq, n_tp, reach), out_shape=p...  38.1 us
    unnamed x1, local copies, waits for them, and re-layouts  0.88 us

profile of v4, /device:TPU:17, one launch (start us, length us, event | category | flops | bytes accessed | tf_op | source)
XLA Modules:
  0.0 39.0 jit_solution(10824968244789396939)
XLA Ops:
  0.0 38.1 %shard_map.55 = bf16[48,8192]{1,0:T(8,128)(2,1)S(1)} custom-call(bf16[192,1024]{1,0:T(8,128)(2,1)} %q_hbm.1, bf16[192,256]{1,0:T(8,128)(2,1)} %k_hbm.1, bf16[192,256]{1,0:T(8,128)(2,1)} %v_hbm.1, s32[12,128]{1,0:T(8,128)} %bitcast.1, bf16[1024,8192]{1,0:T(8,128)(2,1)} %w_hbm.1), custom_call_target="tpu_custom_call" | custom-call | tf_op jit(solution)/shard_map/pallas_call | solution.py:336
  38.1 0.9 %copy.7 = bf16[48,8192]{1,0:T(8,128)(2,1)} copy(bf16[48,8192]{1,0:T(8,128)(2,1)S(1)} %shard_map.55) | data formatting | bytes 1572864

commit v5 on v4

--- a/solution.py
+++ b/solution.py
@@ -16,7 +16,7 @@
 LOG2E = 1.4426950408889634
 SCALE = LOG2E / HD**0.5
 MASKED = -1e30
-CHUNKS = 16
+CHUNKS = 8
 
 
 def kernel(

time: 39.1 us -> 39.1 us (level)
  no operation moved by 1% of the time
where the time goes in v5:
time: 39.1 us; the launch traced here: 38.9 us
  Pallas kernels  38 us (97%)
  local copies, waits for them, and re-layouts  0.88 us (2%)
    pallas_call x1, Pallas kernels, per_device(): pl.pallas_call(functools.partial(kernel, n_seq, n_tp, reach), out_shape=p...  38 us
    unnamed x1, local copies, waits for them, and re-layouts  0.88 us

profile of v5, /device:TPU:17, one launch (start us, length us, event | category | flops | bytes accessed | tf_op | source)
XLA Modules:
  0.0 38.9 jit_solution(14087755295028643154)
XLA Ops:
  0.0 38.0 %shard_map.55 = bf16[48,8192]{1,0:T(8,128)(2,1)S(1)} custom-call(bf16[192,1024]{1,0:T(8,128)(2,1)} %q_hbm.1, bf16[192,256]{1,0:T(8,128)(2,1)} %k_hbm.1, bf16[192,256]{1,0:T(8,128)(2,1)} %v_hbm.1, s32[12,128]{1,0:T(8,128)} %bitcast.1, bf16[1024,8192]{1,0:T(8,128)(2,1)} %w_hbm.1), custom_call_target="tpu_custom_call" | custom-call | tf_op jit(solution)/shard_map/pallas_call | solution.py:336
  38.0 0.9 %copy.7 = bf16[48,8192]{1,0:T(8,128)(2,1)} copy(bf16[48,8192]{1,0:T(8,128)(2,1)S(1)} %shard_map.55) | data formatting | bytes 1572864
